TPU v7x, 32 devices: a whole 2x2x4 slice. The times are simulated.
32 devices in a mesh: tile: 8 (over z, x), sub: 4 (over y, core).
Axes of the slice: x: 2, y: 2, z: 4, core: 2. Of those that a mesh axis runs over, the one named last changes fastest.
Arguments:
- initial_state: float32 [8, 64, 1024], P('tile', None, 'sub'), may hold values from -6 to 6
- cotangent: float32 [8, 64, 1024], P('tile', None, 'sub'), may hold values from -6 to 6
- w_in: bfloat16 [576, 1024], replicated, may hold values from -0.25 to 0.25
- b_in: float32 [1024], replicated, may hold values from -3 to 3
- w_out: bfloat16 [64, 1024], replicated, may hold values from -0.1875 to 0.1875
- edge_flips: int32 [8, 2], P('tile'), may hold values 0 or 1
Outputs:
- final_state: float32 [8, 64, 1024], P('tile', None, 'sub')
- grad_state: float32 [8, 64, 1024], P('tile', None, 'sub')
- grad_w_in: float32 [576, 1024], replicated
- grad_b_in: float32 [1024], replicated
- grad_w_out: float32 [64, 1024], replicated
All inputs are finite; a program needn't handle non-finite values. No bound on the sum of `edge_flips` on one device may be relied on, other than what follows from the above.
Results may differ from a plain program's by a relative error of at most 0.006.
Values may be sent and summed in bfloat16 or wider, within the bound.
A program may use at most 64 MiB of HBM per device.

v0:
```python
import jax
import jax.numpy as jnp
from jax import lax
from jax.sharding import PartitionSpec as P

LEVELS = 64
ROWS = 8
STEPS = 4
TILE_ROW = 4


STEP_SIZE = 0.25


def from_behind(value, axis, by):
    peers = lax.axis_size(axis)
    return lax.ppermute(value, axis, [(i, (i + by) % peers) for i in range(peers)])


def passed_along(value, axis, steps):
    count = lax.axis_size(axis)
    first, last = (max(0, -steps), min(count, count - steps))
    return lax.ppermute(value, axis, [(source, source + steps) for source in range(first, last)])


def level_total(vector):
    return lax.psum(vector, ("tile", "sub"))


def seam_shift():
    sub_count = lax.axis_size("sub")
    return sub_count * TILE_ROW - sub_count + 1


def pad_block(current, flip_north, flip_south, first_sub, last_sub):
    block_width = current.shape[2]
    jump = seam_shift()
    west_col, east_col = [
        from_behind(strip, "tile", offset)
        for strip, offset in ((current[:, :, block_width - 1 :], 1), (current[:, :, :1], -1))
    ]
    extended = jnp.concatenate([west_col, current, east_col], axis=2)
    bottom_row = extended[:, ROWS - 1, :]
    top_row = extended[:, 0, :]
    inner_north, inner_south = [
        passed_along(strip, "sub", offset) for strip, offset in ((bottom_row, 1), (top_row, -1))
    ]
    seam_north, seam_south = [
        from_behind(strip, ("tile", "sub"), offset)
        for strip, offset in ((bottom_row, jump), (top_row, -jump))
    ]
    seam_north = jnp.where(flip_north, seam_north[:, ::-1], seam_north)
    north_row = jnp.where(first_sub, seam_north, inner_north)
    seam_south = jnp.where(flip_south, seam_south[:, ::-1], seam_south)
    south_row = jnp.where(last_sub, seam_south, inner_south)
    return jnp.concatenate([north_row[:, None], extended, south_row[:, None]], axis=1)


def unpad_block(pad_grad, flip_north, flip_south, first_sub, last_sub):
    block_width = pad_grad.shape[2] - 2
    jump = seam_shift()
    extended = pad_grad[:, 1:-1, :]
    north_grad = pad_grad[:, 0, :]
    south_grad = pad_grad[:, -1, :]
    unflip_north = jnp.where(flip_north, north_grad[:, ::-1], north_grad)
    unflip_south = jnp.where(flip_south, south_grad[:, ::-1], south_grad)
    nothing = jnp.zeros_like(north_grad)
    seam_bottom, seam_top = [
        from_behind(strip, ("tile", "sub"), offset)
        for strip, offset in (
            (jnp.where(first_sub, unflip_north, nothing), -jump),
            (jnp.where(last_sub, unflip_south, nothing), jump),
        )
    ]
    inner_bottom, inner_top = [
        passed_along(strip, "sub", offset)
        for strip, offset in (
            (jnp.where(first_sub, nothing, north_grad), -1),
            (jnp.where(last_sub, nothing, south_grad), 1),
        )
    ]
    extended = extended.at[:, ROWS - 1, :].add(seam_bottom + inner_bottom)
    extended = extended.at[:, 0, :].add(seam_top + inner_top)
    inner = extended[:, :, 1:-1]
    from_west, from_east = [
        from_behind(strip, "tile", offset)
        for strip, offset in ((extended[:, :, 0], -1), (extended[:, :, -1], 1))
    ]
    inner = inner.at[:, :, block_width - 1].add(from_west)
    inner = inner.at[:, :, 0].add(from_east)
    return inner


def gather_patches(padded, block_width):
    pieces = [
        padded[:, row_shift : row_shift + ROWS, col_shift : col_shift + block_width]
        for row_shift in range(3)
        for col_shift in range(3)
    ]
    return jnp.stack(pieces, axis=0).reshape(9 * LEVELS, ROWS * block_width)


def scatter_patches(patch_grad, block_width):
    pieces = patch_grad.reshape(9, LEVELS, ROWS, block_width)
    total = jnp.zeros((LEVELS, ROWS + 2, block_width + 2), jnp.float32)
    for row_shift in range(3):
        for col_shift in range(3):
            total = total + jnp.pad(
                pieces[3 * row_shift + col_shift],
                ((0, 0), (row_shift, 2 - row_shift), (col_shift, 2 - col_shift)),
            )
    return total


def shards(initial_state, cotangent, w_in, b_in, w_out, edge_flips):
    block_width = initial_state.shape[2] // ROWS
    total_cols = lax.axis_size("tile") * lax.axis_size("sub") * initial_state.shape[2]
    sub_index = lax.axis_index("sub")
    first_sub = sub_index == 0
    last_sub = sub_index == lax.axis_size("sub") - 1
    flip_north = edge_flips[0, 0] == 1
    flip_south = edge_flips[0, 1] == 1

    def network_input(current):
        padded = pad_block(
            current.astype(jnp.bfloat16), flip_north, flip_south, first_sub, last_sub
        )
        return gather_patches(padded, block_width)

    def first_layer(patch_vals):
        product = lax.dot_general(
            w_in, patch_vals, (((0,), (0,)), ((), ())), preferred_element_type=jnp.float32
        )
        return product + b_in[:, None]

    current = initial_state[0].reshape(LEVELS, ROWS, block_width)
    saved_fields = []
    for step_index in range(STEPS):
        saved_fields.append(current)
        patch_vals = network_input(current)
        pre_act = first_layer(patch_vals)
        hidden_vals = jax.nn.silu(pre_act).astype(jnp.bfloat16)
        tendency = jnp.dot(w_out, hidden_vals, preferred_element_type=jnp.float32)
        level_mean = level_total(jnp.sum(tendency, axis=1)) / total_cols
        current = current + (STEP_SIZE * (tendency - level_mean[:, None])).reshape(current.shape)
    gradient = cotangent[0]
    grad_w_in = jnp.zeros((w_in.shape[0], w_in.shape[1]), jnp.float32)
    grad_w_out = jnp.zeros((w_out.shape[0], w_out.shape[1]), jnp.float32)
    grad_b_in = jnp.zeros((w_in.shape[1],), jnp.float32)
    for step_index in reversed(range(STEPS)):
        scaled = STEP_SIZE * gradient
        level_grad = level_total(jnp.sum(scaled, axis=1)) / total_cols
        tend_grad = (scaled - level_grad[:, None]).astype(jnp.bfloat16)
        patch_vals = network_input(saved_fields[step_index])
        pre_act = first_layer(patch_vals)
        hidden_vals = jax.nn.silu(pre_act).astype(jnp.bfloat16)
        grad_w_out = grad_w_out + lax.dot_general(
            tend_grad, hidden_vals, (((1,), (1,)), ((), ())), preferred_element_type=jnp.float32
        )
        hidden_grad = lax.dot_general(
            w_out, tend_grad, (((0,), (0,)), ((), ())), preferred_element_type=jnp.float32
        )
        sigmoid_vals = jax.nn.sigmoid(pre_act)
        pre_grad = hidden_grad * sigmoid_vals * (1.0 + pre_act * (1.0 - sigmoid_vals))
        grad_b_in = grad_b_in + jnp.sum(pre_grad, axis=1)
        pre_low = pre_grad.astype(jnp.bfloat16)
        grad_w_in = grad_w_in + lax.dot_general(
            patch_vals, pre_low, (((1,), (1,)), ((), ())), preferred_element_type=jnp.float32
        )
        patch_grad = jnp.dot(w_in, pre_low, preferred_element_type=jnp.float32)
        pad_grad = scatter_patches(patch_grad, block_width)
        back_grad = unpad_block(pad_grad, flip_north, flip_south, first_sub, last_sub)
        gradient = gradient + back_grad.reshape(LEVELS, ROWS * block_width)
    quarters = (
        lax.psum_scatter(grad_w_in, "sub", scatter_dimension=1, tiled=True),
        lax.psum_scatter(grad_w_out, "sub", scatter_dimension=1, tiled=True),
        lax.psum_scatter(grad_b_in[None, :], "sub", scatter_dimension=1, tiled=True),
    )
    quarters = lax.psum((quarters[0], quarters[1], quarters[2]), "tile")
    grad_w_in, grad_w_out, bias_row = (
        lax.all_gather(quarters[0].astype(jnp.bfloat16), "sub", axis=1, tiled=True).astype(
            jnp.float32
        ),
        lax.all_gather(quarters[1].astype(jnp.bfloat16), "sub", axis=1, tiled=True).astype(
            jnp.float32
        ),
        lax.all_gather(quarters[2].astype(jnp.bfloat16), "sub", axis=1, tiled=True).astype(
            jnp.float32
        ),
    )
    grad_b_in = bias_row[0]
    final_block = current.reshape(1, LEVELS, ROWS * block_width)
    return (final_block, gradient[None], grad_w_in, grad_b_in, grad_w_out)


def solution(mesh):
    in_specs = (P("tile", None, "sub"), P("tile", None, "sub"), P(), P(), P(), P("tile", None))
    out_specs = (P("tile", None, "sub"), P("tile", None, "sub"), P(), P(), P())
    return jax.shard_map(shards, mesh=mesh, in_specs=in_specs, out_specs=out_specs, check_vma=False)
```

profile of v0, /device:TPU:0, one launch (start us, length us, event | category | flops | bytes accessed | tf_op | source)
XLA Modules:
  0.0 664.1 jit_solution(16025712312118512564)
XLA Ops:
  8.3 3.0 collective-permute-start
  11.3 3.1 collective-permute-start.1
  17.3 3.3 collective-permute-start.4
  23.2 2.2 collective-permute-start.3
  26.8 3.6 collective-permute-done.2
  33.8 40.8 %psum.77 = f32[64]{0:T(128)S(1)} all-reduce(f32[64]{0:T(128)S(1)} %get-tuple-element.323), channel_id=1, replica_groups=mesh['tile'=8,'sub'=4] {'tile','sub'}, use_global_device_ids=true, to_apply=%region_1.2 | all-reduce | flops 64 | bytes 512 | tf_op jit(solution)/shard_map/psum | solution.py:27
  75.3 2.3 collective-permute-start.6
  77.7 2.4 collective-permute-start.7
  83.1 4.1 collective-permute-start.9
  87.2 3.2 collective-permute-start.8
  96.3 42.1 %psum.78 = f32[64]{0:T(128)S(1)} all-reduce(f32[64]{0:T(128)S(1)} %get-tuple-element.327), channel_id=1, replica_groups=mesh['tile'=8,'sub'=4] {'tile','sub'}, use_global_device_ids=true, to_apply=%region_3.4 | all-reduce | flops 64 | bytes 512 | tf_op jit(solution)/shard_map/psum | solution.py:27
  139.0 2.3 collective-permute-start.12
  141.3 2.4 collective-permute-start.13
  150.0 3.6 collective-permute-start.14
  158.4 43.7 %all-reduce.37 = (f32[64]{0:T(128)S(1)}, f32[64]{0:T(128)S(1)}) all-reduce(f32[64]{0:T(128)S(1)} %get-tuple-element.331, f32[64]{0:T(128)S(1)} %fusion.26), channel_id=1, replica_groups=mesh['tile'=8,'sub'=4] {'tile','sub'}, use_global_device_ids=true, to_apply=%region_5.6 | all-reduce | flops 128 | bytes 1024 | tf_op jit(solution)/shard_map/psum | solution.py:27
  202.3 2.3 collective-permute-start.18
  204.6 2.4 collective-permute-start.19
  210.0 3.8 collective-permute-start.21
  213.9 3.7 collective-permute-start.20
  250.2 3.2 collective-permute-start.27
  253.4 3.6 collective-permute-start.26
  257.0 2.3 collective-permute-done.26
  259.3 4.1 collective-permute-start.28
  265.3 6.3 collective-permute-done.29
  272.3 36.8 %psum.82 = f32[64]{0:T(128)S(1)} all-reduce(f32[64]{0:T(128)S(1)} %get-tuple-element.214), channel_id=1, replica_groups=mesh['tile'=8,'sub'=4] {'tile','sub'}, use_global_device_ids=true, to_apply=%region_11.12 | all-reduce | flops 64 | bytes 512 | tf_op jit(solution)/shard_map/psum | solution.py:27
  333.0 2.9 collective-permute-start.30
  337.3 3.0 fusion.17
  340.3 4.5 collective-permute-start.33
  345.7 4.1 collective-permute-done.32
  358.9 4.6 collective-permute-done.35
  365.9 36.9 %psum.83 = f32[64]{0:T(128)} all-reduce(f32[64]{0:T(128)S(1)} %multiply_reduce_fusion.1), channel_id=1, replica_groups=mesh['tile'=8,'sub'=4] {'tile','sub'}, use_global_device_ids=true, to_apply=%region_13.14 | all-reduce | flops 64 | bytes 512 | tf_op jit(solution)/shard_map/psum | solution.py:27
  404.4 2.4 fusion.76
  428.9 2.9 collective-permute-start.36
  434.5 4.4 collective-permute-start.39
  439.7 4.2 collective-permute-done.38
  449.6 5.1 collective-permute-done.41
  458.0 37.1 %all-reduce.36 = (f32[64]{0:T(128)}, f32[64]{0:T(128)}) all-reduce(f32[64]{0:T(128)} %get-tuple-element.335, f32[64]{0:T(128)S(1)} %multiply_reduce_fusion), channel_id=1, replica_groups=mesh['tile'=8,'sub'=4] {'tile','sub'}, use_global_device_ids=true, to_apply=%region_7.8 | all-reduce | flops 128 | bytes 1024 | tf_op jit(solution)/shard_map/psum | solution.py:27
  496.8 2.6 fusion.75
  509.7 2.8 collective-permute-start.42
  513.8 9.5 %reduce-scatter.10.cloned.1.call-done = f32[256,1]{1,0:T(8,128)} async-done(((f32[1024,1]{1,0:T(8,128)}), f32[256,1]{1,0:T(8,128)}) %reduce-scatter.10.cloned.1.call-update) | async-done | bytes 1040
  524.3 21.9 %reduce-scatter.8.cloned.1.call-done = f32[64,256]{1,0:T(8,128)} async-done(((f32[64,1024]{1,0:T(8,128)}), f32[64,256]{1,0:T(8,128)}) %reduce-scatter.8.cloned.1.call-update) | async-done | bytes 65552 | tf_op jit(solution)/shard_map/reduce_scatter | solution.py:176
  546.2 35.9 %reduce-scatter.6.cloned.1.call-done = f32[576,256]{1,0:T(8,128)} async-done(((f32[576,1024]{1,0:T(8,128)}), f32[576,256]{1,0:T(8,128)}) %reduce-scatter.6.cloned.1.call-update) | async-done | bytes 589840 | tf_op jit(solution)/shard_map/reduce_scatter | solution.py:175
  582.1 44.4 %all-reduce.40 = (bf16[576,256]{1,0:T(8,128)(2,1)}, bf16[1,256]{1,0:T(2,128)(2,1)S(1)}, bf16[64,256]{1,0:T(8,128)(2,1)S(1)}) all-reduce(f32[576,256]{1,0:T(8,128)} %reduce-scatter.6.cloned.1.call-done, f32[1,256]{1,0:T(1,128)S(1)} %copy.248, f32[64,256]{1,0:T(8,128)} %reduce-scatter.8.cloned.1.call-done), channel_id=1, replica_groups=mesh['tile'=8,'sub'=4] {'tile'}, use_global_device_ids=true, to_apply=%region_17.18 | all-reduce | flops 164096 | bytes 984576 | tf_op jit(solution)/shard_map/psum | solution.py:179
  628.7 4.2 collective-permute-done.44
  636.6 5.3 collective-permute-done.47
  642.8 5.1 all_gather.10
  648.5 5.4 all_gather.11
  654.6 3.0 convert_element_type.174
  (413 shorter events, 164.3 us)
Async XLA Ops:
  7.2 516.1 %reduce-scatter.10.cloned.1.call-start = ((), (), s32[]{:S(2)}) async-start(), calls=%async_computation.6 | async-start | bytes 655360
  8.3 7.6 %collective-permute-start = (bf16[64,8,1]{0,2,1:T(2,128)(2,1)S(1)}, bf16[64,8,1]{0,2,1:T(2,128)(2,1)S(1)}, u32[]{:S(2)}, u32[]{:S(2)}) collective-permute-start(bf16[64,8,1]{0,2,1:T(2,128)(2,1)S(1)} %get-tuple-element.317), channel_id=1, source_target_pairs={{0,4},{4,8},{8,12},{12,16},{16,20},{20,24},{24,28},{28,0},{1,5},{5... | collective-permute-start | bytes 3080 | tf_op jit(solution)/shard_map/ppermute | solution.py:17
  11.3 4.6 collective-permute-start.1
  16.0 10.8 %collective-permute-start.5 = (bf16[64,34]{0,1:T(8,128)(2,1)S(1)}, bf16[64,34]{0,1:T(8,128)(2,1)S(1)}, u32[]{:S(2)}, u32[]{:S(2)}) collective-permute-start(bf16[64,34]{0,1:T(8,128)(2,1)S(1)} %get-tuple-element.309), channel_id=1, source_target_pairs={{1,0},{2,1},{3,2},{5,4},{6,5},{7,6},{9,8},{10,9},{11,10},{13,12},{... | collective-permute-start | bytes 13064 | tf_op jit(solution)/shard_map/ppermute | solution.py:23
  17.3 9.5 %collective-permute-start.4 = (bf16[64,34]{0,1:T(8,128)(2,1)S(1)}, bf16[64,34]{0,1:T(8,128)(2,1)S(1)}, u32[]{:S(2)}, u32[]{:S(2)}) collective-permute-start(bf16[64,34]{0,1:T(8,128)(2,1)S(1)} %get-tuple-element.309), channel_id=1, source_target_pairs={{0,19},{1,20},{2,21},{3,22},{4,23},{5,24},{6,25},{7,26},{8,27},{9,... | collective-permute-start | bytes 13064 | tf_op jit(solution)/shard_map/ppermute | solution.py:17
  23.2 7.2 %collective-permute-start.3 = (bf16[64,34]{0,1:T(8,128)(2,1)S(1)}, bf16[64,34]{0,1:T(8,128)(2,1)S(1)}, u32[]{:S(2)}, u32[]{:S(2)}) collective-permute-start(bf16[64,34]{0,1:T(8,128)(2,1)S(1)} %get-tuple-element.310), channel_id=1, source_target_pairs={{0,1},{1,2},{2,3},{4,5},{5,6},{6,7},{8,9},{9,10},{10,11},{12,13},{... | collective-permute-start | bytes 13064 | tf_op jit(solution)/shard_map/ppermute | solution.py:23
  25.4 4.9 collective-permute-start.2
  75.3 6.4 collective-permute-start.6
  77.7 4.0 collective-permute-start.7
  81.7 8.7 %collective-permute-start.10 = (bf16[64,34]{0,1:T(8,128)(2,1)S(1)}, bf16[64,34]{0,1:T(8,128)(2,1)S(1)}, u32[]{:S(2)}, u32[]{:S(2)}) collective-permute-start(bf16[64,34]{0,1:T(8,128)(2,1)S(1)} %get-tuple-element.305), channel_id=1, source_target_pairs={{0,19},{1,20},{2,21},{3,22},{4,23},{5,24},{6,25},{7,26},{8,27},{9,... | collective-permute-start | bytes 13064 | tf_op jit(solution)/shard_map/ppermute | solution.py:17
  81.8 8.7 %collective-permute-start.11 = (bf16[64,34]{0,1:T(8,128)(2,1)S(1)}, bf16[64,34]{0,1:T(8,128)(2,1)S(1)}, u32[]{:S(2)}, u32[]{:S(2)}) collective-permute-start(bf16[64,34]{0,1:T(8,128)(2,1)S(1)} %get-tuple-element.305), channel_id=1, source_target_pairs={{1,0},{2,1},{3,2},{5,4},{6,5},{7,6},{9,8},{10,9},{11,10},{13,12},{... | collective-permute-start | bytes 13064 | tf_op jit(solution)/shard_map/ppermute | solution.py:23
  83.1 9.1 %collective-permute-start.9 = (bf16[64,34]{0,1:T(8,128)(2,1)S(1)}, bf16[64,34]{0,1:T(8,128)(2,1)S(1)}, u32[]{:S(2)}, u32[]{:S(2)}) collective-permute-start(bf16[64,34]{0,1:T(8,128)(2,1)S(1)} %get-tuple-element.306), channel_id=1, source_target_pairs={{0,1},{1,2},{2,3},{4,5},{5,6},{6,7},{8,9},{9,10},{10,11},{12,13},{... | collective-permute-start | bytes 13064 | tf_op jit(solution)/shard_map/ppermute | solution.py:23
  87.2 4.9 collective-permute-start.8
  139.0 6.4 collective-permute-start.12
  145.4 8.2 %collective-permute-start.17 = (bf16[64,34]{0,1:T(8,128)(2,1)S(1)}, bf16[64,34]{0,1:T(8,128)(2,1)S(1)}, u32[]{:S(2)}, u32[]{:S(2)}) collective-permute-start(bf16[64,34]{0,1:T(8,128)(2,1)S(1)} %get-tuple-element.301), channel_id=1, source_target_pairs={{1,0},{2,1},{3,2},{5,4},{6,5},{7,6},{9,8},{10,9},{11,10},{13,12},{... | collective-permute-start | bytes 13064 | tf_op jit(solution)/shard_map/ppermute | solution.py:23
  146.7 6.9 %collective-permute-start.16 = (bf16[64,34]{0,1:T(8,128)(2,1)S(1)}, bf16[64,34]{0,1:T(8,128)(2,1)S(1)}, u32[]{:S(2)}, u32[]{:S(2)}) collective-permute-start(bf16[64,34]{0,1:T(8,128)(2,1)S(1)} %get-tuple-element.301), channel_id=1, source_target_pairs={{0,19},{1,20},{2,21},{3,22},{4,23},{5,24},{6,25},{7,26},{8,27},{9,... | collective-permute-start | bytes 13064 | tf_op jit(solution)/shard_map/ppermute | solution.py:17
  148.5 6.5 collective-permute-start.15
  150.0 5.0 collective-permute-start.14
  202.3 6.4 collective-permute-start.18
  204.6 4.0 collective-permute-start.19
  208.7 8.9 %collective-permute-start.22 = (bf16[64,34]{0,1:T(8,128)(2,1)S(1)}, bf16[64,34]{0,1:T(8,128)(2,1)S(1)}, u32[]{:S(2)}, u32[]{:S(2)}) collective-permute-start(bf16[64,34]{0,1:T(8,128)(2,1)S(1)} %get-tuple-element.297), channel_id=1, source_target_pairs={{0,19},{1,20},{2,21},{3,22},{4,23},{5,24},{6,25},{7,26},{8,27},{9,... | collective-permute-start | bytes 13064 | tf_op jit(solution)/shard_map/ppermute | solution.py:17
  208.7 8.9 %collective-permute-start.23 = (bf16[64,34]{0,1:T(8,128)(2,1)S(1)}, bf16[64,34]{0,1:T(8,128)(2,1)S(1)}, u32[]{:S(2)}, u32[]{:S(2)}) collective-permute-start(bf16[64,34]{0,1:T(8,128)(2,1)S(1)} %get-tuple-element.297), channel_id=1, source_target_pairs={{1,0},{2,1},{3,2},{5,4},{6,5},{7,6},{9,8},{10,9},{11,10},{13,12},{... | collective-permute-start | bytes 13064 | tf_op jit(solution)/shard_map/ppermute | solution.py:23
  210.0 9.0 %collective-permute-start.21 = (bf16[64,34]{0,1:T(8,128)(2,1)S(1)}, bf16[64,34]{0,1:T(8,128)(2,1)S(1)}, u32[]{:S(2)}, u32[]{:S(2)}) collective-permute-start(bf16[64,34]{0,1:T(8,128)(2,1)S(1)} %get-tuple-element.298), channel_id=1, source_target_pairs={{0,1},{1,2},{2,3},{4,5},{5,6},{6,7},{8,9},{9,10},{10,11},{12,13},{... | collective-permute-start | bytes 13064 | tf_op jit(solution)/shard_map/ppermute | solution.py:23
  213.9 5.1 collective-permute-start.20
  245.4 11.6 %collective-permute-start.24 = (f32[64,34]{0,1:T(8,128)S(1)}, f32[64,34]{0,1:T(8,128)S(1)}, u32[]{:S(2)}, u32[]{:S(2)}) collective-permute-start(f32[64,34]{0,1:T(8,128)S(1)} %get-tuple-element.279), channel_id=1, source_target_pairs={{0,19},{1,20},{2,21},{3,22},{4,23},{5,24},{6,25},{7,26},{8,27},{9,... | collective-permute-start | bytes 26120 | tf_op jit(solution)/shard_map/ppermute | solution.py:17
  246.9 10.1 %collective-permute-start.25 = (f32[64,34]{0,1:T(8,128)S(1)}, f32[64,34]{0,1:T(8,128)S(1)}, u32[]{:S(2)}, u32[]{:S(2)}) collective-permute-start(f32[64,34]{0,1:T(8,128)S(1)} %get-tuple-element.280), channel_id=1, source_target_pairs={{1,0},{2,1},{3,2},{5,4},{6,5},{7,6},{9,8},{10,9},{11,10},{13,12},{... | collective-permute-start | bytes 26120 | tf_op jit(solution)/shard_map/ppermute | solution.py:23
  250.2 6.8 %collective-permute-start.27 = (f32[64,34]{0,1:T(8,128)S(1)}, f32[64,34]{0,1:T(8,128)S(1)}, u32[]{:S(2)}, u32[]{:S(2)}) collective-permute-start(f32[64,34]{0,1:T(8,128)S(1)} %get-tuple-element.278), channel_id=1, source_target_pairs={{0,1},{1,2},{2,3},{4,5},{5,6},{6,7},{8,9},{9,10},{10,11},{12,13},{... | collective-permute-start | bytes 26120 | tf_op jit(solution)/shard_map/ppermute | solution.py:23
  253.4 6.0 collective-permute-start.26
  259.3 5.9 collective-permute-start.28
  265.2 6.4 collective-permute-start.29
  333.0 12.0 %collective-permute-start.30 = (f32[64,34]{0,1:T(8,128)S(1)}, f32[64,34]{0,1:T(8,128)S(1)}, u32[]{:S(2)}, u32[]{:S(2)}) collective-permute-start(f32[64,34]{0,1:T(8,128)S(1)} %get-tuple-element.273), channel_id=1, source_target_pairs={{0,19},{1,20},{2,21},{3,22},{4,23},{5,24},{6,25},{7,26},{8,27},{9,... | collective-permute-start | bytes 26120 | tf_op jit(solution)/shard_map/ppermute | solution.py:17
  335.9 9.1 %collective-permute-start.31 = (f32[64,34]{0,1:T(8,128)S(1)}, f32[64,34]{0,1:T(8,128)S(1)}, u32[]{:S(2)}, u32[]{:S(2)}) collective-permute-start(f32[64,34]{0,1:T(8,128)S(1)} %get-tuple-element.274), channel_id=1, source_target_pairs={{1,0},{2,1},{3,2},{5,4},{6,5},{7,6},{9,8},{10,9},{11,10},{13,12},{... | collective-permute-start | bytes 26120 | tf_op jit(solution)/shard_map/ppermute | solution.py:23
  340.3 5.4 collective-permute-start.33
  344.8 5.1 collective-permute-start.32
  352.8 4.7 collective-permute-start.34
  357.1 6.4 collective-permute-start.35
  428.9 10.7 %collective-permute-start.36 = (f32[64,34]{0,1:T(8,128)S(1)}, f32[64,34]{0,1:T(8,128)S(1)}, u32[]{:S(2)}, u32[]{:S(2)}) collective-permute-start(f32[64,34]{0,1:T(8,128)S(1)} %get-tuple-element.267), channel_id=1, source_target_pairs={{0,19},{1,20},{2,21},{3,22},{4,23},{5,24},{6,25},{7,26},{8,27},{9,... | collective-permute-start | bytes 26120 | tf_op jit(solution)/shard_map/ppermute | solution.py:17
  431.8 7.8 %collective-permute-start.37 = (f32[64,34]{0,1:T(8,128)S(1)}, f32[64,34]{0,1:T(8,128)S(1)}, u32[]{:S(2)}, u32[]{:S(2)}) collective-permute-start(f32[64,34]{0,1:T(8,128)S(1)} %get-tuple-element.268), channel_id=1, source_target_pairs={{1,0},{2,1},{3,2},{5,4},{6,5},{7,6},{9,8},{10,9},{11,10},{13,12},{... | collective-permute-start | bytes 26120 | tf_op jit(solution)/shard_map/ppermute | solution.py:23
  434.5 5.2 collective-permute-start.39
  438.9 5.1 collective-permute-start.38
  448.2 6.6 collective-permute-start.41
  500.5 45.6 %reduce-scatter.8.cloned.1.call-start = ((), (), s32[]{:S(2)}) async-start(), calls=%async_computation.5 | async-start | bytes 327680 | tf_op jit(solution)/shard_map/reduce_scatter | solution.py:176
  502.7 79.4 %reduce-scatter.6.cloned.1.call-start = ((), (), s32[]{:S(2)}) async-start(), calls=%async_computation.3 | async-start | bytes 2949120 | tf_op jit(solution)/shard_map/reduce_scatter | solution.py:175
  506.8 147.7 %all-gather.2.cloned.1.call-start = ((), (), s32[]{:S(2)}) async-start(), calls=%async_computation.4 | async-start | bytes 1474560 | tf_op jit(solution)/shard_map/all_gather | solution.py:181
  509.7 118.2 %collective-permute-start.42 = (f32[64,34]{0,1:T(8,128)S(1)}, f32[64,34]{0,1:T(8,128)S(1)}, u32[]{:S(2)}, u32[]{:S(2)}) collective-permute-start(f32[64,34]{0,1:T(8,128)S(1)} %get-tuple-element.261), channel_id=1, source_target_pairs={{0,19},{1,20},{2,21},{3,22},{4,23},{5,24},{6,25},{7,26},{8,27},{9,... | collective-permute-start | bytes 26120 | tf_op jit(solution)/shard_map/ppermute | solution.py:17
  512.5 115.5 %collective-permute-start.43 = (f32[64,34]{0,1:T(8,128)S(1)}, f32[64,34]{0,1:T(8,128)S(1)}, u32[]{:S(2)}, u32[]{:S(2)}) collective-permute-start(f32[64,34]{0,1:T(8,128)S(1)} %get-tuple-element.262), channel_id=1, source_target_pairs={{1,0},{2,1},{3,2},{5,4},{6,5},{7,6},{9,8},{10,9},{11,10},{13,12},{... | collective-permute-start | bytes 26120 | tf_op jit(solution)/shard_map/ppermute | solution.py:23
  627.9 5.1 collective-permute-start.44
  635.6 6.4 collective-permute-start.47
  (61 other events, 2151.7 us)
Sparse Core Ops, SparseCore 0:
  500.7 22.5 reduce-scatter.9
  526.3 19.8 reduce-scatter.7
  549.3 32.7 reduce-scatter.5
  626.6 15.1 all-gather.1
where the time goes:
time: 668 us; the launch traced here: 664 us
  blocking collectives  292 us (44%)
  waiting for transfers between devices  119 us (18%)
  starting transfers between devices  97.9 us (15%)
  local copies, waits for them, and re-layouts  82.4 us (12%)
  matrix products  32.2 us (5%)
  other arithmetic  23.4 us (4%)
  between operations  16.5 us (2%)
    psum x6, blocking collectives, level_total(): return lax.psum(vector, ('tile', 'sub'))  237 us
    ppermute x32, starting transfers between devices, from_behind(): lax.ppermute(value, axis, [(i, (i + by) % peers) for i in range(peers)])  62.4 us
    ppermute x32, waiting for transfers between devices, from_behind(): lax.ppermute(value, axis, [(i, (i + by) % peers) for i in range(peers)])  51.1 us
    slice x40, local copies, waits for them, and re-layouts, scatter_patches(): pieces[3 * row_shift + col_shift]  46.4 us
    psum x1, blocking collectives, shards(): quarters = lax.psum((quarters[0], quarters[1], quarters[2]), 'tile')  44.4 us
    reduce_scatter x1, waiting for transfers between devices, shards(): lax.psum_scatter(grad_w_in, 'sub', scatter_dimension=1, tiled=True)  35.9 us
    ppermute x16, starting transfers between devices, passed_along(): lax.ppermute(value, axis, [(source, source + steps) for source in range(f...  35.3 us
    reduce_scatter x1, waiting for transfers between devices, shards(): lax.psum_scatter(grad_w_out, 'sub', scatter_dimension=1, tiled=True)  21.9 us
  transfers between devices with their start and end apart: 52, of which 22 were waited for; matrix products, arithmetic and copies ran while one was open for 4% of the time, Pallas kernels for 0%

commit v1 on v0

v1 whole, which is shorter than its diff:
```python
import functools

import jax
import jax.numpy as jnp
from jax import lax
from jax.experimental import pallas as pl
from jax.experimental.pallas import tpu as pltpu
from jax.sharding import PartitionSpec as P

STEPS = 4
TILE_ROW = 4
STEP_SIZE = 0.25
LEAD = 8
MESH = pl.DeviceIdType.MESH
F32 = jnp.float32
BF16 = jnp.bfloat16

PIECES = {}
TOTAL_ROWS = 0


def layout(width, rows):
    names = [("N", width), ("S", width), ("W", rows), ("E", rows)]
    names += [(name, 8) for name in ("NW", "NE", "SW", "SE")]
    place, at = {}, 0
    for name, size in names:
        place[name] = (at, size)
        at += size
    return place, at


def dot(a, b, dims, precision=None):
    return lax.dot_general(a, b, (dims, ((), ())), preferred_element_type=F32, precision=precision)


def chain_kernel(
    tiles, subs, rows, width, levels, hidden,
    state_ref, cot_ref, w_in_ref, b_in_ref, w_out_ref, flips_ref,
    final_ref, grad_ref, gw_in_ref, gb_ref, gw_out_ref,
    send, recv, tile_out, tile_in, sub_out, sub_in,
    padded, pad_grad, edge, field, gradient, totals, pre, hid, slope, patch,
    gp16, gt16,
    halo_ssem, halo_rsem, tile_ssem, tile_rsem, sub_ssem, sub_rsem,
):
    place, _ = layout(width, rows)
    cols = rows * width
    inv_total = 1.0 / (tiles * subs * cols)
    me_t, me_s = lax.axis_index("tile"), lax.axis_index("sub")
    first, last = me_s == 0, me_s == subs - 1
    wide = width + 2 * LEAD

    def tile_at(by):
        return lax.rem(me_t + by + 2 * tiles, tiles)

    def north_of(by):
        return (jnp.where(first, tile_at(by - TILE_ROW), tile_at(by)), jnp.where(first, subs - 1, me_s - 1))

    def south_of(by):
        return (jnp.where(last, tile_at(by + TILE_ROW), tile_at(by)), jnp.where(last, 0, me_s + 1))

    targets = {
        "N": north_of(0), "S": south_of(0), "W": (tile_at(-1), me_s), "E": (tile_at(1), me_s),
        "NW": north_of(-1), "NE": north_of(1), "SW": south_of(-1), "SE": south_of(1),
    }

    def halo_copies(p):
        out = []
        for i, (name, (at, size)) in enumerate(place.items()):
            out.append(pltpu.make_async_remote_copy(
                src_ref=send.at[p, pl.ds(at, size)], dst_ref=recv.at[p, pl.ds(at, size)],
                send_sem=halo_ssem.at[p, i], recv_sem=halo_rsem.at[p, i],
                device_id=targets[name], device_id_type=MESH))
        return out

    def tile_copies(p):
        return [pltpu.make_async_remote_copy(
            src_ref=tile_out.at[p], dst_ref=tile_in.at[p, d - 1],
            send_sem=tile_ssem.at[p, d - 1], recv_sem=tile_rsem.at[p, d - 1],
            device_id=(tile_at(d), me_s), device_id_type=MESH) for d in range(1, tiles)]

    def sub_copies(p):
        return [pltpu.make_async_remote_copy(
            src_ref=sub_out.at[p], dst_ref=sub_in.at[p, d - 1],
            send_sem=sub_ssem.at[p, d - 1], recv_sem=sub_rsem.at[p, d - 1],
            device_id=(me_t, lax.rem(me_s + d, subs)), device_id_type=MESH) for d in range(1, subs)]

    def start_exchange(p):
        for copy in tile_copies(p) + halo_copies(p):
            copy.start()

    def finish_exchange(p):
        for copy in tile_copies(p):
            copy.wait()
        total = tile_out[p]
        for d in range(1, tiles):
            total = total + tile_in[p, d - 1]
        sub_out[p] = total
        for copy in sub_copies(p):
            copy.start()
        for copy in halo_copies(p):
            copy.wait()
        for copy in sub_copies(p):
            copy.wait()
        for d in range(1, subs):
            total = total + sub_in[p, d - 1]
        return total

    at_row = lax.broadcasted_iota(jnp.int32, (wide, wide), 0)
    at_col = lax.broadcasted_iota(jnp.int32, (wide, wide), 1)
    same = (at_row == at_col).astype(F32)
    turned = (at_row + at_col == wide - 1).astype(F32)

    def seam_matrix(flag, here):
        mix = jnp.where(here, flag, 0).astype(F32)
        return turned * mix + same * (1.0 - mix)

    turn_north = seam_matrix(flips_ref[0, 0], first)
    turn_south = seam_matrix(flips_ref[0, 1], last)

    def send_field(p):
        for name, row in (("N", 0), ("S", rows - 1)):
            at = place[name][0]
            line = field[row * width:(row + 1) * width]
            send[p, at:at + width] = line
            for side, cell in (("W", 0), ("E", width - 1)):
                corner = place[name + side][0]
                send[p, corner:corner + 1] = line[cell:cell + 1]
        for name, cell in (("W", 0), ("E", width - 1)):
            at = place[name][0]
            for r in range(rows):
                send[p, at + r:at + r + 1] = field[r * width + cell:r * width + cell + 1]

    def pad_field(p, shift):
        padded[1:rows + 1, LEAD:LEAD + width, :] = (field[...]).reshape(rows, width, levels)
        for name, cell in (("E", LEAD - 1), ("W", LEAD + width)):
            at = place[name][0]
            for r in range(rows):
                padded[r + 1, cell:cell + 1] = recv[p, at + r:at + r + 1] - shift
        for name, row, turn in (("S", 0, turn_north), ("N", rows + 1, turn_south)):
            at = place[name][0]
            edge[LEAD:LEAD + width] = recv[p, at:at + width] - shift
            for side, cell in (("E", LEAD - 1), ("W", LEAD + width)):
                corner = place[name + side][0]
                edge[cell:cell + 1] = recv[p, corner:corner + 1] - shift
            padded[row] = dot(turn.astype(BF16), edge[...].astype(BF16), ((1,), (0,)))

    send[...] = jnp.zeros_like(send)
    tile_out[...] = jnp.zeros_like(tile_out)
    edge[...] = jnp.zeros_like(edge)
    field[...] = state_ref[0].T
    gradient[...] = cot_ref[0].T
    send_field(0)
    tile_out[0, 1:2] = jnp.sum(gradient[...], axis=0, keepdims=True)
    start_exchange(0)
    gw_in_ref[...] = jnp.zeros_like(gw_in_ref)
    gb_ref[...] = jnp.zeros_like(gb_ref)
    gw_out_ref[...] = jnp.zeros_like(gw_out_ref)
    padded[...] = jnp.zeros_like(padded)

    def forward(k, carry):
        total = finish_exchange(k)
        shift = total[0:1] * (STEP_SIZE * inv_total)
        field[...] = field[...] - shift

        @pl.when(k == 0)
        def _():
            totals[...] = total

        pad_field(k, shift)
        for a in range(3):
            for b in range(3):
                o = 3 * a + b
                piece = padded[a:a + rows, LEAD - 1 + b:LEAD - 1 + b + width, :]
                patch[k, :, o * levels:(o + 1) * levels] = piece.reshape(cols, levels).astype(BF16)
        act = dot(patch[k], w_in_ref[...], ((1,), (0,))) + b_in_ref[...]
        pre[...] = act
        low = (act * jax.nn.sigmoid(act)).astype(BF16)
        hid[k] = low
        tendency = dot(low, w_out_ref[...], ((1,), (1,)))
        field[...] = field[...] + STEP_SIZE * tendency
        tile_out[k + 1, 0:1] = jnp.sum(tendency, axis=0, keepdims=True)

        @pl.when(k < STEPS - 1)
        def _():
            send_field(k + 1)
            start_exchange(k + 1)

        value = pre[...]
        sig = jax.nn.sigmoid(value)
        slope[k] = sig * (1.0 + value * (1.0 - sig))
        return carry

    lax.fori_loop(0, STEPS, forward, 0)

    def backward(j, carry):
        k = STEPS - 1 - j
        p = STEPS + j
        level_grad = totals[1:2] * (STEP_SIZE * inv_total)
        low_gt = (STEP_SIZE * gradient[...] - level_grad).astype(BF16)
        gt16[...] = low_gt
        gh = dot(low_gt, w_out_ref[...], ((1,), (0,)))
        gp = gh * slope[k]
        pre[...] = gp
        low = gp.astype(BF16)
        gp16[...] = low
        gi = dot(low, w_in_ref[...], ((1,), (1,)))
        pad_grad[...] = jnp.zeros_like(pad_grad)
        for a in range(3):
            for b in range(3):
                o = 3 * a + b
                piece = gi[:, o * levels:(o + 1) * levels].reshape(rows, width, levels)
                pad_grad[a:a + rows, LEAD - 1 + b:LEAD - 1 + b + width, :] += piece
        whole = jnp.sum(gi, axis=0, keepdims=True)
        part = whole[:, 0:levels]
        for o in range(1, 9):
            part = part + whole[:, o * levels:(o + 1) * levels]
        tile_out[p, 1:2] = part
        for name, row, turn in (("N", 0, turn_north), ("S", rows + 1, turn_south)):
            at = place[name][0]
            edge[...] = dot(turn, pad_grad[row], ((1,), (0,)), lax.Precision.HIGHEST)
            send[p, at:at + width] = edge[LEAD:LEAD + width]
            for side, cell in (("W", LEAD - 1), ("E", LEAD + width)):
                corner = place[name + side][0]
                send[p, corner:corner + 1] = edge[cell:cell + 1]
        for name, cell in (("W", LEAD - 1), ("E", LEAD + width)):
            at = place[name][0]
            for r in range(rows):
                send[p, at + r:at + r + 1] = pad_grad[r + 1, cell:cell + 1]
        start_exchange(p)
        gradient[...] += pad_grad[1:rows + 1, LEAD:LEAD + width, :].reshape(cols, levels)
        gw_in_ref[...] += dot(patch[k], gp16[...], ((0,), (0,)))
        gw_out_ref[...] += dot(gt16[...], hid[k], ((0,), (0,)))
        gb_ref[...] += jnp.sum(pre[...], axis=0, keepdims=True)
        total = finish_exchange(p)

        @pl.when(j == 0)
        def _():
            field[...] = field[...] - total[0:1] * (STEP_SIZE * inv_total)

        totals[1:2] = totals[1:2] + total[1:2]
        for name, row in (("N", rows - 1), ("S", 0)):
            at = place[name][0]
            gradient[row * width:(row + 1) * width] += recv[p, at:at + width]
            for side, cell in (("W", width - 1), ("E", 0)):
                corner = place[name + side][0]
                gradient[row * width + cell:row * width + cell + 1] += recv[p, corner:corner + 1]
        for name, cell in (("W", width - 1), ("E", 0)):
            at = place[name][0]
            for r in range(rows):
                gradient[r * width + cell:r * width + cell + 1] += recv[p, at + r:at + r + 1]
        return carry

    lax.fori_loop(0, STEPS, backward, 0)
    final_ref[0] = field[...].T
    grad_ref[0] = gradient[...].T


def shards(tiles, subs, initial_state, cotangent, w_in, b_in, w_out, edge_flips):
    _, levels, cols = initial_state.shape
    in_width, hidden = w_in.shape
    side = 1
    while side * side < cols * subs:
        side += 1
    rows, width = side // subs, side
    _, buffer_rows = layout(width, rows)
    phases = 2 * STEPS
    wide = width + 2 * LEAD
    vmem = pl.BlockSpec(memory_space=pltpu.VMEM)
    final, grad, gw_in, gb, gw_out = pl.pallas_call(
        functools.partial(chain_kernel, tiles, subs, rows, width, levels, hidden),
        out_shape=(
            jax.ShapeDtypeStruct(initial_state.shape, F32),
            jax.ShapeDtypeStruct(initial_state.shape, F32),
            jax.ShapeDtypeStruct((in_width, hidden), F32),
            jax.ShapeDtypeStruct((1, hidden), F32),
            jax.ShapeDtypeStruct((levels, hidden), F32),
        ),
        in_specs=[vmem] * 5 + [pl.BlockSpec(memory_space=pltpu.SMEM)],
        out_specs=[vmem] * 5,
        scratch_shapes=[
            pltpu.VMEM((phases, buffer_rows, levels), F32),
            pltpu.VMEM((phases, buffer_rows, levels), F32),
            pltpu.VMEM((phases, 8, levels), F32),
            pltpu.VMEM((phases, tiles - 1, 8, levels), F32),
            pltpu.VMEM((phases, 8, levels), F32),
            pltpu.VMEM((phases, subs - 1, 8, levels), F32),
            pltpu.VMEM((rows + 2, wide, levels), F32),
            pltpu.VMEM((rows + 2, wide, levels), F32),
            pltpu.VMEM((wide, levels), F32),
            pltpu.VMEM((cols, levels), F32),
            pltpu.VMEM((cols, levels), F32),
            pltpu.VMEM((8, levels), F32),
            pltpu.VMEM((cols, hidden), F32),
            pltpu.VMEM((STEPS, cols, hidden), BF16),
            pltpu.VMEM((STEPS, cols, hidden), F32),
            pltpu.VMEM((STEPS, cols, in_width), BF16),
            pltpu.VMEM((cols, hidden), BF16),
            pltpu.VMEM((cols, levels), BF16),
            pltpu.SemaphoreType.DMA((phases, 8)),
            pltpu.SemaphoreType.DMA((phases, 8)),
            pltpu.SemaphoreType.DMA((phases, tiles - 1)),
            pltpu.SemaphoreType.DMA((phases, tiles - 1)),
            pltpu.SemaphoreType.DMA((phases, subs - 1)),
            pltpu.SemaphoreType.DMA((phases, subs - 1)),
        ],
        compiler_params=pltpu.CompilerParams(has_side_effects=True, vmem_limit_bytes=48 * 1024 * 1024),
        name="chain",
    )(initial_state, cotangent, w_in, b_in[None, :], w_out, edge_flips)
    stacked = jnp.concatenate([gw_in, gw_out, gb, jnp.zeros((7, hidden), F32)], axis=0)
    part = lax.psum_scatter(stacked, "sub", scatter_dimension=1, tiled=True)
    part = lax.psum(part, "tile")
    full = lax.all_gather(part.astype(BF16), "sub", axis=1, tiled=True).astype(F32)
    return (final, grad, full[:in_width], full[in_width + levels], full[in_width:in_width + levels])


def solution(mesh):
    in_specs = (P("tile", None, "sub"), P("tile", None, "sub"), P(), P(), P(), P("tile", None))
    out_specs = (P("tile", None, "sub"), P("tile", None, "sub"), P(), P(), P())
    body = functools.partial(shards, mesh.shape["tile"], mesh.shape["sub"])
    return jax.shard_map(body, mesh=mesh, in_specs=in_specs, out_specs=out_specs, check_vma=False)
```

time: 668 us -> 199 us (0.30)
  blocking collectives: 292 us -> 44.4 us
  starting transfers between devices: 97.9 us -> 0.08 us
  Pallas kernels: 0 us -> 74.1 us
  local copies, waits for them, and re-layouts: 82.4 us -> 12.4 us
  waiting for transfers between devices: 119 us -> 51.2 us
  matrix products: 32.2 us -> 0 us
  other arithmetic: 23.4 us -> 1.76 us
    psum x7 -> x1, blocking collectives: 282 us -> 44.4 us  [shards(): part = lax.psum(part, 'tile')]
    ppermute x48 -> x0, starting transfers between devices: 97.8 us -> none  [the longest x32 62.4 us: from_behind(): lax.ppermute(value, axis, [(i, (i + by) % peers) for i in range(peers)])]
    pallas_call x0 -> x1, Pallas kernels: none -> 74.1 us  [shards(): pl.pallas_call(functools.partial(chain_kernel, tiles, subs, rows, width,...]
    ppermute x48 -> x0, waiting for transfers between devices: 51.9 us -> none  [the longest x32 51.1 us: from_behind(): lax.ppermute(value, axis, [(i, (i + by) % peers) for i in range(peers)])]
    slice x59 -> x3, local copies, waits for them, and re-layouts: 50.1 us -> 5.89 us  [the longest x1 2.96 us: shards(): full[:in_width]]
    dot_general x24 -> x0, matrix products: 32.2 us -> none  [the longest x4 7.46 us: shards(): lax.dot_general(w_out, tend_grad, (((0,), (0,)), ((), ())), preferred_ele...]
    reduce_scatter x2 -> x1, waiting for transfers between devices: 57.8 us -> 35.1 us  [shards(): part = lax.psum_scatter(stacked, 'sub', scatter_dimension=1, tiled=True)]
    all_gather x1, waiting for transfers between devices: 0.01 us -> 16.1 us  [shards(): lax.all_gather(part.astype(BF16), 'sub', axis=1, tiled=True).astype(F32)]
  transfers between devices with their start and end apart: 52 -> 2, of which waited for: 22 -> 2; matrix products, arithmetic and copies ran while one was open for 4% -> 0% of each run, Pallas kernels for 0% -> 0%
where the time goes in v1:
time: 199 us; the launch traced here: 198 us
  Pallas kernels  74.1 us (37%)
  waiting for transfers between devices  51.2 us (26%)
  blocking collectives  44.4 us (22%)
  between operations  14.1 us (7%)
  local copies, waits for them, and re-layouts  12.4 us (6%)
    pallas_call x1, Pallas kernels, shards(): pl.pallas_call(functools.partial(chain_kernel, tiles, subs, rows, width,...  74.1 us
    psum x1, blocking collectives, shards(): part = lax.psum(part, 'tile')  44.4 us
    reduce_scatter x1, waiting for transfers between devices, shards(): part = lax.psum_scatter(stacked, 'sub', scatter_dimension=1, tiled=True)  35.1 us
    all_gather x1, waiting for transfers between devices, shards(): lax.all_gather(part.astype(BF16), 'sub', axis=1, tiled=True).astype(F32)  16.1 us
    unnamed x14, local copies, waits for them, and re-layouts  6.45 us
  transfers between devices with their start and end apart: 2, of which 2 were waited for; matrix products, arithmetic and copies ran while one was open for 0% of the time, Pallas kernels for 0%

profile of v1, /device:TPU:0, one launch (start us, length us, event | category | flops | bytes accessed | tf_op | source)
XLA Modules:
  0.0 198.1 jit_solution(13062417664900867835)
XLA Ops:
  7.2 0.0 reduce-scatter.2.cloned.1.call-start
  7.2 0.1 pad.3.clone
  7.3 0.0 copy-start
  7.3 1.3 copy-done
  8.6 0.0 copy-start.1
  8.6 0.9 copy-done.1
  9.5 0.0 copy-start.2
  9.5 0.8 copy-done.2
  10.3 0.0 copy-start.3
  10.3 0.8 copy-done.3
  11.2 0.0 copy-start.4
  11.2 0.7 copy-done.4
  11.8 0.0 copy-start.5
  11.8 0.7 copy-done.5
  12.5 74.1 %chain.1 = (f32[1,64,256]{2,1,0:T(8,128)S(1)}, f32[1,64,256]{2,1,0:T(8,128)S(1)}, f32[576,1024]{1,0:T(8,128)S(1)}, f32[1,1024]{1,0:T(1,128)S(1)}, f32[64,1024]{1,0:T(8,128)S(1)}) custom-call(f32[1,64,256]{2,1,0:T(8,128)S(1)} %copy-done.2, f32[1,64,256]{2,1,0:T(8,128)S(1)} %copy-done.3, bf16[576,1024]{1,0:T(8,128)(2,1)S(1)} %copy-done, ...), custom_call_target="tpu_custom_call" | custom-call | tf_op jit(solution)/shard_map/chain/pallas_call | solution.py:269
  86.6 1.8 maximum_maximum_fusion
  88.4 0.0 reduce-scatter.2.cloned.1.call-update
  88.4 0.0 all-gather.2.cloned.1.call-start
  88.5 35.1 %reduce-scatter.2.cloned.1.call-done = f32[648,256]{1,0:T(8,128)} async-done(((f32[648,1024]{1,0:T(8,128)}), f32[648,256]{1,0:T(8,128)}) %reduce-scatter.2.cloned.1.call-update) | async-done | bytes 663568 | tf_op jit(solution)/shard_map/reduce_scatter | solution.py:310
  123.5 44.4 %all-reduce.1 = bf16[648,256]{1,0:T(8,128)(2,1)} all-reduce(f32[648,256]{1,0:T(8,128)} %reduce-scatter.2.cloned.1.call-done), channel_id=1, replica_groups=mesh['tile'=8,'sub'=4] {'tile'}, use_global_device_ids=true, to_apply=%region_1.0 | all-reduce | flops 165888 | bytes 995328 | tf_op jit(solution)/shard_map/psum | solution.py:311
  167.9 0.0 all-gather.2.cloned.1.call-update
  168.0 16.1 %all-gather.2.cloned.1.call-done = bf16[648,1024]{1,0:T(8,128)(2,1)} async-done(((bf16[648,256]{1,0:T(8,128)(2,1)}), bf16[648,1024]{1,0:T(8,128)(2,1)}) %all-gather.2.cloned.1.call-update) | async-done | bytes 1327120 | tf_op jit(solution)/shard_map/all_gather | solution.py:312
  184.1 1.3 slice.13
  185.4 1.6 slice.14
  187.0 3.0 %slice.12 = f32[576,1024]{1,0:T(8,128)} slice(bf16[648,1024]{1,0:T(8,128)(2,1)} %all-gather.2.cloned.1.call-done), slice={[0:576], [0:1024]} | slice | bytes 4718592 | tf_op jit(solution)/shard_map/slice | solution.py:313
  190.0 0.6 copy.15
  190.6 0.6 copy.16
  (1 shorter events, 0.0 us)
Async XLA Ops:
  7.2 116.3 %reduce-scatter.2.cloned.1.call-start = ((), (), s32[]{:S(2)}) async-start(), calls=%async_computation.1 | async-start | bytes 3317760 | tf_op jit(solution)/shard_map/reduce_scatter | solution.py:310
  7.3 1.3 copy-start
  8.6 0.9 copy-start.1
  9.5 0.8 copy-start.2
  10.3 0.8 copy-start.3
  11.2 0.7 copy-start.4
  11.8 0.7 copy-start.5
  88.4 95.7 %all-gather.2.cloned.1.call-start = ((), (), s32[]{:S(2)}) async-start(), calls=%async_computation.2 | async-start | bytes 1658880 | tf_op jit(solution)/shard_map/all_gather | solution.py:312
Sparse Core Ops, SparseCore 0:
  88.5 34.9 reduce-scatter.1
  168.1 15.9 all-gather.1

commit v2 on v1

--- a/solution.py
+++ b/solution.py
@@ -15,8 +15,8 @@
 F32 = jnp.float32
 BF16 = jnp.bfloat16
 
-PIECES = {}
-TOTAL_ROWS = 0
+LANES = 128
+DIRECT_LIMIT = 64
 
 
 def layout(width, rows):
@@ -29,6 +29,22 @@
     return place, at
 
 
+def reduce_plan(tiles, subs, flat_rows):
+    bits = [("sub", 1 << i) for i in range(subs.bit_length() - 1)]
+    bits += [("tile", 1 << i) for i in range(tiles.bit_length() - 1)]
+    unit = 16 * tiles * subs
+    units = -(-flat_rows // unit)
+    count = min(3, units)
+    groups, at = [], 0
+    for g in range(count):
+        size = (units // count + (1 if g < units % count else 0)) * unit
+        turning = bits[1:4]
+        order = bits[:1] + turning[g:] + turning[:g] + bits[4:]
+        groups.append((at, size, order))
+        at += size
+    return groups, at
+
+
 def dot(a, b, dims, precision=None):
     return lax.dot_general(a, b, (dims, ((), ())), preferred_element_type=F32, precision=precision)
 
@@ -37,6 +53,8 @@
     tiles, subs, rows, width, levels, hidden,
     state_ref, cot_ref, w_in_ref, b_in_ref, w_out_ref, flips_ref,
     final_ref, grad_ref, gw_in_ref, gb_ref, gw_out_ref,
+    flat, out_half, in_half, whole, red_ssem, red_rsem, gat_ssem, gat_rsem,
+    bias_out, bias_tiles, bias_subs, bias_ssem, bias_rsem, side_ssem, side_rsem,
     send, recv, tile_out, tile_in, sub_out, sub_in,
     padded, pad_grad, edge, field, gradient, totals, pre, hid, slope, patch,
     gp16, gt16,
@@ -72,11 +90,22 @@
                 device_id=targets[name], device_id_type=MESH))
         return out
 
-    def tile_copies(p):
-        return [pltpu.make_async_remote_copy(
-            src_ref=tile_out.at[p], dst_ref=tile_in.at[p, d - 1],
-            send_sem=tile_ssem.at[p, d - 1], recv_sem=tile_rsem.at[p, d - 1],
-            device_id=(tile_at(d), me_s), device_id_type=MESH) for d in range(1, tiles)]
+    direct = tiles * subs <= DIRECT_LIMIT
+    me = me_t * subs + me_s
+
+    def sum_copies(p):
+        out = []
+        for d in range(1, tiles * subs if direct else tiles):
+            if direct:
+                peer = lax.rem(me + d, tiles * subs)
+                there = (peer // subs, lax.rem(peer, subs))
+            else:
+                there = (tile_at(d), me_s)
+            out.append(pltpu.make_async_remote_copy(
+                src_ref=tile_out.at[p], dst_ref=tile_in.at[p, d - 1],
+                send_sem=tile_ssem.at[p, d - 1], recv_sem=tile_rsem.at[p, d - 1],
+                device_id=there, device_id_type=MESH))
+        return out
 
     def sub_copies(p):
         return [pltpu.make_async_remote_copy(
@@ -85,24 +114,26 @@
             device_id=(me_t, lax.rem(me_s + d, subs)), device_id_type=MESH) for d in range(1, subs)]
 
     def start_exchange(p):
-        for copy in tile_copies(p) + halo_copies(p):
+        for copy in sum_copies(p) + halo_copies(p):
             copy.start()
 
     def finish_exchange(p):
-        for copy in tile_copies(p):
+        for copy in sum_copies(p):
             copy.wait()
         total = tile_out[p]
-        for d in range(1, tiles):
+        for d in range(1, tiles * subs if direct else tiles):
             total = total + tile_in[p, d - 1]
-        sub_out[p] = total
-        for copy in sub_copies(p):
-            copy.start()
+        if not direct:
+            sub_out[p] = total
+            for copy in sub_copies(p):
+                copy.start()
         for copy in halo_copies(p):
             copy.wait()
-        for copy in sub_copies(p):
-            copy.wait()
-        for d in range(1, subs):
-            total = total + sub_in[p, d - 1]
+        if not direct:
+            for copy in sub_copies(p):
+                copy.wait()
+            for d in range(1, subs):
+                total = total + sub_in[p, d - 1]
         return total
 
     at_row = lax.broadcasted_iota(jnp.int32, (wide, wide), 0)
@@ -210,10 +241,10 @@
                 o = 3 * a + b
                 piece = gi[:, o * levels:(o + 1) * levels].reshape(rows, width, levels)
                 pad_grad[a:a + rows, LEAD - 1 + b:LEAD - 1 + b + width, :] += piece
-        whole = jnp.sum(gi, axis=0, keepdims=True)
-        part = whole[:, 0:levels]
+        gi_sum = jnp.sum(gi, axis=0, keepdims=True)
+        part = gi_sum[:, 0:levels]
         for o in range(1, 9):
-            part = part + whole[:, o * levels:(o + 1) * levels]
+            part = part + gi_sum[:, o * levels:(o + 1) * levels]
         tile_out[p, 1:2] = part
         for name, row, turn in (("N", 0, turn_north), ("S", rows + 1, turn_south)):
             at = place[name][0]
@@ -251,6 +282,118 @@
         return carry
 
     lax.fori_loop(0, STEPS, backward, 0)
+
+    in_width = gw_in_ref.shape[0]
+    stride = in_width + levels
+    for c in range(hidden // LANES):
+        bias_out[0, c:c + 1] = gb_ref[:, c * LANES:(c + 1) * LANES]
+    bias_tiles[me_t] = bias_out[0]
+
+    def bias_tile_copies():
+        return [pltpu.make_async_remote_copy(
+            src_ref=bias_out.at[0], dst_ref=bias_tiles.at[me_t],
+            send_sem=bias_ssem.at[d - 1], recv_sem=bias_rsem.at[d - 1],
+            device_id=(tile_at(d), me_s), device_id_type=MESH) for d in range(1, tiles)]
+
+    def bias_sub_copies():
+        return [pltpu.make_async_remote_copy(
+            src_ref=bias_out.at[1], dst_ref=bias_subs.at[me_s],
+            send_sem=side_ssem.at[d - 1], recv_sem=side_rsem.at[d - 1],
+            device_id=(me_t, lax.rem(me_s + d, subs)), device_id_type=MESH) for d in range(1, subs)]
+
+    for copy in bias_tile_copies():
+        copy.start()
+    groups, flat_rows = reduce_plan(tiles, subs, stride * (hidden // LANES))
+    for c in range(hidden // LANES):
+        at, lanes = c * stride, slice(c * LANES, (c + 1) * LANES)
+        flat[at:at + in_width] = gw_in_ref[:, lanes]
+        flat[at + in_width:at + in_width + levels] = gw_out_ref[:, lanes]
+    used = stride * (hidden // LANES)
+    if flat_rows > used:
+        flat[used:flat_rows] = jnp.zeros((flat_rows - used, LANES), F32)
+
+    def bit_of(axis, step):
+        index = me_t if axis == "tile" else me_s
+        return lax.rem(index // step, 2)
+
+    def peer_of(axis, step):
+        if axis == "tile":
+            return (me_t + step * (1 - 2 * bit_of(axis, step)), me_s)
+        return (me_t, me_s + step * (1 - 2 * bit_of(axis, step)))
+
+    def bases(group):
+        start, size, order = group
+        out, base = [], start
+        for axis, step in order:
+            out.append((base, size // 2))
+            size = size // 2
+            base = base + bit_of(axis, step) * size
+        return out, base, size
+
+    depth = len(groups[0][2])
+
+    def reduce_copy(g, i):
+        start, size, order = groups[g]
+        half = size >> (i + 1)
+        at = start + size - (size >> i)
+        return pltpu.make_async_remote_copy(
+            src_ref=out_half.at[pl.ds(at, half)], dst_ref=in_half.at[pl.ds(at, half)],
+            send_sem=red_ssem.at[g, i], recv_sem=red_rsem.at[g, i],
+            device_id=peer_of(*order[i]), device_id_type=MESH)
+
+    def gather_copy(g, i):
+        start, size, order = groups[g]
+        part = size >> (i + 1)
+        base = bases(groups[g])[0][i][0] + bit_of(*order[i]) * part
+        rows_here = pl.ds(pl.multiple_of(base, 16), part)
+        return pltpu.make_async_remote_copy(
+            src_ref=whole.at[rows_here], dst_ref=whole.at[rows_here],
+            send_sem=gat_ssem.at[g, i], recv_sem=gat_rsem.at[g, i],
+            device_id=peer_of(*order[i]), device_id_type=MESH)
+
+    for i in range(depth + 1):
+        for g, (start, size, order) in enumerate(groups):
+            levels_of = bases((start, size, order))
+            if i > 0:
+                reduce_copy(g, i - 1).wait()
+                base, half = levels_of[0][i - 1]
+                at = start + size - (size >> (i - 1))
+                kept = pl.ds(pl.multiple_of(base + bit_of(*order[i - 1]) * half, 16), half)
+                flat[kept] = flat[kept] + in_half[at:at + half].astype(F32)
+            if i < depth:
+                base, half = levels_of[0][i]
+                at = start + size - (size >> i)
+                away = pl.ds(pl.multiple_of(base + (1 - bit_of(*order[i])) * half, 16), half)
+                out_half[at:at + half] = flat[away].astype(BF16)
+                reduce_copy(g, i).start()
+            else:
+                own = pl.ds(pl.multiple_of(levels_of[1], 16), levels_of[2])
+                whole[own] = flat[own].astype(BF16)
+                gather_copy(g, depth - 1).start()
+    for copy in bias_tile_copies():
+        copy.wait()
+    bias = bias_tiles[0]
+    for d in range(1, tiles):
+        bias = bias + bias_tiles[d]
+    bias_out[1] = bias
+    bias_subs[me_s] = bias
+    for copy in bias_sub_copies():
+        copy.start()
+    for i in reversed(range(depth)):
+        for g in range(len(groups)):
+            gather_copy(g, i).wait()
+            if i > 0:
+                gather_copy(g, i - 1).start()
+    for copy in bias_sub_copies():
+        copy.wait()
+    bias = bias_subs[0]
+    for d in range(1, subs):
+        bias = bias + bias_subs[d]
+    for c in range(hidden // LANES):
+        at, lanes = c * stride, slice(c * LANES, (c + 1) * LANES)
+        gw_in_ref[:, lanes] = whole[at:at + in_width].astype(F32)
+        gw_out_ref[:, lanes] = whole[at + in_width:at + in_width + levels].astype(F32)
+        gb_ref[:, lanes] = bias[c:c + 1]
     final_ref[0] = field[...].T
     grad_ref[0] = gradient[...].T
 
@@ -264,6 +407,9 @@
     rows, width = side // subs, side
     _, buffer_rows = layout(width, rows)
     phases = 2 * STEPS
+    groups, flat_rows = reduce_plan(tiles, subs, (in_width + levels) * (hidden // LANES))
+    depth = len(groups[0][2])
+    fan = tiles * subs - 1 if tiles * subs <= DIRECT_LIMIT else tiles - 1
     wide = width + 2 * LEAD
     vmem = pl.BlockSpec(memory_space=pltpu.VMEM)
     final, grad, gw_in, gb, gw_out = pl.pallas_call(
@@ -278,10 +424,25 @@
         in_specs=[vmem] * 5 + [pl.BlockSpec(memory_space=pltpu.SMEM)],
         out_specs=[vmem] * 5,
         scratch_shapes=[
+            pltpu.VMEM((flat_rows, LANES), F32),
+            pltpu.VMEM((flat_rows, LANES), BF16),
+            pltpu.VMEM((flat_rows, LANES), BF16),
+            pltpu.VMEM((flat_rows, LANES), BF16),
+            pltpu.SemaphoreType.DMA((len(groups), depth)),
+            pltpu.SemaphoreType.DMA((len(groups), depth)),
+            pltpu.SemaphoreType.DMA((len(groups), depth)),
+            pltpu.SemaphoreType.DMA((len(groups), depth)),
+            pltpu.VMEM((2, hidden // LANES, LANES), F32),
+            pltpu.VMEM((tiles, hidden // LANES, LANES), F32),
+            pltpu.VMEM((subs, hidden // LANES, LANES), F32),
+            pltpu.SemaphoreType.DMA((tiles - 1,)),
+            pltpu.SemaphoreType.DMA((tiles - 1,)),
+            pltpu.SemaphoreType.DMA((subs - 1,)),
+            pltpu.SemaphoreType.DMA((subs - 1,)),
             pltpu.VMEM((phases, buffer_rows, levels), F32),
             pltpu.VMEM((phases, buffer_rows, levels), F32),
             pltpu.VMEM((phases, 8, levels), F32),
-            pltpu.VMEM((phases, tiles - 1, 8, levels), F32),
+            pltpu.VMEM((phases, fan, 8, levels), F32),
             pltpu.VMEM((phases, 8, levels), F32),
             pltpu.VMEM((phases, subs - 1, 8, levels), F32),
             pltpu.VMEM((rows + 2, wide, levels), F32),
@@ -298,19 +459,15 @@
             pltpu.VMEM((cols, levels), BF16),
             pltpu.SemaphoreType.DMA((phases, 8)),
             pltpu.SemaphoreType.DMA((phases, 8)),
-            pltpu.SemaphoreType.DMA((phases, tiles - 1)),
-            pltpu.SemaphoreType.DMA((phases, tiles - 1)),
+            pltpu.SemaphoreType.DMA((phases, fan)),
+            pltpu.SemaphoreType.DMA((phases, fan)),
             pltpu.SemaphoreType.DMA((phases, subs - 1)),
             pltpu.SemaphoreType.DMA((phases, subs - 1)),
         ],
         compiler_params=pltpu.CompilerParams(has_side_effects=True, vmem_limit_bytes=48 * 1024 * 1024),
         name="chain",
     )(initial_state, cotangent, w_in, b_in[None, :], w_out, edge_flips)
-    stacked = jnp.concatenate([gw_in, gw_out, gb, jnp.zeros((7, hidden), F32)], axis=0)
-    part = lax.psum_scatter(stacked, "sub", scatter_dimension=1, tiled=True)
-    part = lax.psum(part, "tile")
-    full = lax.all_gather(part.astype(BF16), "sub", axis=1, tiled=True).astype(F32)
-    return (final, grad, full[:in_width], full[in_width + levels], full[in_width:in_width + levels])
+    return (final, grad, gw_in, gb[0], gw_out)
 
 
 def solution(mesh):

time: 199 us -> 118 us (0.59)
  waiting for transfers between devices: 51.2 us -> 0 us
  blocking collectives: 44.4 us -> 0 us
  Pallas kernels: 74.1 us -> 108 us
  between operations: 14.1 us -> 0.66 us
  local copies, waits for them, and re-layouts: 12.4 us -> 9.15 us
    psum x1 -> x0, blocking collectives: 44.4 us -> none  [shards(): part = lax.psum(part, 'tile')]
    reduce_scatter x1 -> x0, waiting for transfers between devices: 35.1 us -> none  [shards(): part = lax.psum_scatter(stacked, 'sub', scatter_dimension=1, tiled=True)]
    pallas_call x1, Pallas kernels: 74.1 us -> 108 us  [shards(): pl.pallas_call(functools.partial(chain_kernel, tiles, subs, rows, width,...]
    all_gather x1 -> x0, waiting for transfers between devices: 16.1 us -> none  [shards(): lax.all_gather(part.astype(BF16), 'sub', axis=1, tiled=True).astype(F32)]
    slice x3 -> x0, local copies, waits for them, and re-layouts: 5.89 us -> none  [the longest x1 2.96 us: shards(): full[:in_width]]
    unnamed x14 -> x17, local copies, waits for them, and re-layouts: 6.45 us -> 9.15 us
  transfers between devices with their start and end apart: 2 -> 0, of which waited for: 2 -> 0; matrix products, arithmetic and copies ran while one was open for 0% -> 0% of each run, Pallas kernels for 0% -> 0%
where the time goes in v2:
time: 118 us
  Pallas kernels  108 us (92%)
  local copies, waits for them, and re-layouts  9.15 us (8%)
    pallas_call x1, Pallas kernels, shards(): pl.pallas_call(functools.partial(chain_kernel, tiles, subs, rows, width,...  108 us
    unnamed x17, local copies, waits for them, and re-layouts  9.15 us

profile of v2, /device:TPU:0, one launch (start us, length us, event | category | flops | bytes accessed | tf_op | source)
XLA Modules:
  0.0 117.5 jit_solution(17111652656411015073)
XLA Ops:
  0.6 0.0 copy-start
  0.6 1.3 %copy-done = bf16[576,1024]{1,0:T(8,128)(2,1)S(1)} copy-done((bf16[576,1024]{1,0:T(8,128)(2,1)S(1)}, bf16[576,1024]{1,0:T(8,128)(2,1)}, u32[]{:S(2)}) %copy-start) | copy-done | bytes 1179672
  1.9 0.0 copy-start.1
  1.9 0.9 copy-done.1
  2.8 0.0 copy-start.2
  2.8 0.8 copy-done.2
  3.6 0.0 copy-start.3
  3.7 0.8 copy-done.3
  4.5 0.0 copy-start.4
  4.5 0.7 copy-done.4
  5.2 0.0 copy-start.5
  5.2 0.7 copy-done.5
  5.8 107.7 %chain.1 = (f32[1,64,256]{2,1,0:T(8,128)S(1)}, f32[1,64,256]{2,1,0:T(8,128)S(1)}, f32[576,1024]{1,0:T(8,128)S(1)}, f32[1,1024]{1,0:T(1,128)S(1)}, f32[64,1024]{1,0:T(8,128)S(1)}) custom-call(f32[1,64,256]{2,1,0:T(8,128)S(1)} %copy-done.2, f32[1,64,256]{2,1,0:T(8,128)S(1)} %copy-done.3, bf16[576,1024]{1,0:T(8,128)(2,1)S(1)} %copy-done, ...), custom_call_target="tpu_custom_call" | custom-call | tf_op jit(solution)/shard_map/chain/pallas_call | solution.py:415
  113.6 0.6 copy.16
  114.2 0.6 copy.17
  114.8 1.4 %copy.18 = f32[576,1024]{1,0:T(8,128)} copy(f32[576,1024]{1,0:T(8,128)S(1)} %get-tuple-element.22) | data formatting | bytes 4718592
  116.2 0.6 copy.19
  116.8 0.7 copy.20
Async XLA Ops:
  0.6 1.3 %copy-start = (bf16[576,1024]{1,0:T(8,128)(2,1)S(1)}, bf16[576,1024]{1,0:T(8,128)(2,1)}, u32[]{:S(2)}) copy-start(bf16[576,1024]{1,0:T(8,128)(2,1)} %w_in_ref.1) | copy-start | bytes 3538948
  1.9 0.9 copy-start.1
  2.8 0.8 copy-start.2
  3.6 0.8 copy-start.3
  4.5 0.7 copy-start.4
  5.2 0.7 copy-start.5

commit v3 on v2

--- a/solution.py
+++ b/solution.py
@@ -51,8 +51,9 @@
 
 def chain_kernel(
     tiles, subs, rows, width, levels, hidden,
-    state_ref, cot_ref, w_in_ref, b_in_ref, w_out_ref, flips_ref,
+    state_hbm, cot_hbm, w_in_hbm, b_in_hbm, w_out_hbm, flips_ref,
     final_ref, grad_ref, gw_in_ref, gb_ref, gw_out_ref,
+    state_ref, cot_ref, w_in_ref, b_in_ref, w_out_ref, load_sem,
     flat, out_half, in_half, whole, red_ssem, red_rsem, gat_ssem, gat_rsem,
     bias_out, bias_tiles, bias_subs, bias_ssem, bias_rsem, side_ssem, side_rsem,
     send, recv, tile_out, tile_in, sub_out, sub_in,
@@ -175,9 +176,16 @@
                 edge[cell:cell + 1] = recv[p, corner:corner + 1] - shift
             padded[row] = dot(turn.astype(BF16), edge[...].astype(BF16), ((1,), (0,)))
 
+    pairs = ((state_hbm, state_ref), (cot_hbm, cot_ref), (b_in_hbm, b_in_ref),
+             (w_out_hbm, w_out_ref), (w_in_hbm, w_in_ref))
+    loads = [pltpu.make_async_copy(a, b, load_sem.at[i]) for i, (a, b) in enumerate(pairs)]
+    for load in loads:
+        load.start()
     send[...] = jnp.zeros_like(send)
     tile_out[...] = jnp.zeros_like(tile_out)
     edge[...] = jnp.zeros_like(edge)
+    loads[0].wait()
+    loads[1].wait()
     field[...] = state_ref[0].T
     gradient[...] = cot_ref[0].T
     send_field(0)
@@ -187,6 +195,9 @@
     gb_ref[...] = jnp.zeros_like(gb_ref)
     gw_out_ref[...] = jnp.zeros_like(gw_out_ref)
     padded[...] = jnp.zeros_like(padded)
+
+    for load in loads[2:]:
+        load.wait()
 
     def forward(k, carry):
         total = finish_exchange(k)
@@ -421,9 +432,15 @@
             jax.ShapeDtypeStruct((1, hidden), F32),
             jax.ShapeDtypeStruct((levels, hidden), F32),
         ),
-        in_specs=[vmem] * 5 + [pl.BlockSpec(memory_space=pltpu.SMEM)],
+        in_specs=[pl.BlockSpec(memory_space=pltpu.HBM)] * 5 + [pl.BlockSpec(memory_space=pltpu.SMEM)],
         out_specs=[vmem] * 5,
         scratch_shapes=[
+            pltpu.VMEM(initial_state.shape, F32),
+            pltpu.VMEM(cotangent.shape, F32),
+            pltpu.VMEM(w_in.shape, BF16),
+            pltpu.VMEM((1, hidden), F32),
+            pltpu.VMEM(w_out.shape, BF16),
+            pltpu.SemaphoreType.DMA((5,)),
             pltpu.VMEM((flat_rows, LANES), F32),
             pltpu.VMEM((flat_rows, LANES), BF16),
             pltpu.VMEM((flat_rows, LANES), BF16),

time: 118 us -> 119 us (level)
  no operation moved by 1% of the time
where the time goes in v3:
time: 119 us; the launch traced here: 118 us
  Pallas kernels  108 us (91%)
  local copies, waits for them, and re-layouts  9.15 us (8%)
    pallas_call x1, Pallas kernels, shards(): pl.pallas_call(functools.partial(chain_kernel, tiles, subs, rows, width,...  108 us
    unnamed x17, local copies, waits for them, and re-layouts  9.15 us

profile of v3, /device:TPU:0, one launch (start us, length us, event | category | flops | bytes accessed | tf_op | source)
XLA Modules:
  0.0 118.3 jit_solution(8838647264996744179)
XLA Ops:
  0.6 0.0 copy-start
  0.6 1.3 %copy-done = bf16[576,1024]{1,0:T(8,128)(2,1)S(1)} copy-done((bf16[576,1024]{1,0:T(8,128)(2,1)S(1)}, bf16[576,1024]{1,0:T(8,128)(2,1)}, u32[]{:S(2)}) %copy-start) | copy-done | bytes 1179672
  1.9 0.0 copy-start.1
  1.9 0.9 copy-done.1
  2.8 0.0 copy-start.2
  2.8 0.8 copy-done.2
  3.6 0.0 copy-start.3
  3.7 0.8 copy-done.3
  4.5 0.0 copy-start.4
  4.5 0.7 copy-done.4
  5.2 0.0 copy-start.5
  5.2 0.7 copy-done.5
  5.8 108.5 %chain.1 = (f32[1,64,256]{2,1,0:T(8,128)S(1)}, f32[1,64,256]{2,1,0:T(8,128)S(1)}, f32[576,1024]{1,0:T(8,128)S(1)}, f32[1,1024]{1,0:T(1,128)S(1)}, f32[64,1024]{1,0:T(8,128)S(1)}) custom-call(f32[1,64,256]{2,1,0:T(8,128)S(1)} %copy-done.2, f32[1,64,256]{2,1,0:T(8,128)S(1)} %copy-done.3, bf16[576,1024]{1,0:T(8,128)(2,1)S(1)} %copy-done, ...), custom_call_target="tpu_custom_call" | custom-call | tf_op jit(solution)/shard_map/chain/pallas_call | solution.py:426
  114.3 0.6 copy.16
  114.9 0.6 copy.17
  115.6 1.4 %copy.18 = f32[576,1024]{1,0:T(8,128)} copy(f32[576,1024]{1,0:T(8,128)S(1)} %get-tuple-element.22) | data formatting | bytes 4718592
  117.0 0.6 copy.19
  117.6 0.7 copy.20
Async XLA Ops:
  0.6 1.3 %copy-start = (bf16[576,1024]{1,0:T(8,128)(2,1)S(1)}, bf16[576,1024]{1,0:T(8,128)(2,1)}, u32[]{:S(2)}) copy-start(bf16[576,1024]{1,0:T(8,128)(2,1)} %w_in_hbm.1) | copy-start | bytes 3538948
  1.9 0.9 copy-start.1
  2.8 0.8 copy-start.2
  3.6 0.8 copy-start.3
  4.5 0.7 copy-start.4
  5.2 0.7 copy-start.5
